TPU v7x, 128 devices: a whole 4x4x4 slice. The times are simulated.
128 devices in a mesh: dp: 1, ty: 16 (over z, y), tx: 8 (over x, core).
Axes of the slice: x: 4, y: 4, z: 4, core: 2. Of those that a mesh axis runs over, the one named last changes fastest.
Arguments:
- hidden: bfloat16 [8192, 2048], P(('dp', 'ty'), 'tx')
- positions: int32 [8192], P(('dp', 'tx'))
- g_ffn: bfloat16 [2048], P('tx')
- w_gate: bfloat16 [2048, 8192], P('tx', 'ty')
- w_up: bfloat16 [2048, 8192], P('tx', 'ty')
- w_down: bfloat16 [8192, 2048], P('ty', 'tx')
- g_attn: bfloat16 [2048], P('tx')
- w_q: bfloat16 [2048, 32, 64], P('tx', 'ty')
- w_kv: bfloat16 [2048, 16, 64], P('tx', 'ty')
- grad_h2: bfloat16 [8192, 2048], P(('dp', 'ty'), 'tx')
- grad_q: bfloat16 [8192, 32, 64], P(('dp', 'tx'), 'ty')
- grad_kv: bfloat16 [8192, 16, 64], P(('dp', 'tx'), 'ty')
Outputs:
- output 1: bfloat16 [8192, 2048], P(('dp', 'ty'), 'tx')
- output 2: bfloat16 [8192, 32, 64], P(('dp', 'tx'), 'ty')
- output 3: bfloat16 [8192, 16, 64], P(('dp', 'tx'), 'ty')
- output 4: bfloat16 [8192, 2048], P(('dp', 'ty'), 'tx')
- output 5: float32 [2048], P(('dp', 'tx'))
- output 6: float32 [2048], P(('dp', 'tx'))
- output 7: float32 [2048, 8192], P(('dp', 'tx'), 'ty')
- output 8: float32 [2048, 8192], P(('dp', 'tx'), 'ty')
- output 9: float32 [8192, 2048], P(('dp', 'ty'), 'tx')
- output 10: float32 [2048, 32, 64], P(('dp', 'tx'), 'ty')
- output 11: float32 [2048, 16, 64], P(('dp', 'tx'), 'ty')
All inputs are finite; a program needn't handle non-finite values.
Results may differ from a plain program's by a relative error of at most 0.02.
Values are sent between devices in bfloat16 or wider.
A program may use at most 1 GiB of HBM per device.

v0:
```python
import jax
import jax.numpy as jnp
import numpy as np
from jax import lax
from jax.experimental import pallas as pl
from jax.experimental.pallas import tpu as pltpu
from jax.sharding import PartitionSpec as P

NORM_EPS = 1e-5
ROPE_BASE = 10000.0
RING = 4
TY = 16
TX = 8
NN = (((1,), (0,)), ((), ()))
TN = (((0,), (0,)), ((), ()))
NT = (((1,), (1,)), ((), ()))
BF16 = jnp.bfloat16
F32 = jnp.float32
ORDER = (2, 3, 1, 0)
SPREAD = (0, 3, 1, 2)
BOTH = (0, 1)
SIDES = ((0, 1), (1, -1))
MESH = pl.DeviceIdType.MESH


def wrap(value, size=RING):
    return lax.rem(value + 2 * size, size)


def aligned(start, size, unit=16):
    return pl.ds(pl.multiple_of(start, unit), size)


def chunk(index, size):
    return aligned(index * size, size, size)


def dot(a, b, form):
    return lax.dot_general(a, b, form, preferred_element_type=F32)


class Place:
    def __init__(self):
        self.ty = lax.axis_index("ty")
        self.tx = lax.axis_index("tx")
        self.coord = {"z": self.ty // RING, "y": lax.rem(self.ty, RING), "x": self.tx // 2}
        self.core = lax.rem(self.tx, 2)
        self.sibling = {"tx": self.tx + 1 - 2 * self.core}

    def peer(self, axis, delta):
        c = wrap(self.coord[axis] + delta)
        if axis == "x":
            return {"tx": c * 2 + self.core}
        if axis == "z":
            return {"ty": c * RING + self.coord["y"]}
        return {"ty": self.coord["z"] * RING + c}

    def slot(self, axis, delta, other_axis, other_delta):
        c = {axis: wrap(self.coord[axis] + delta), other_axis: wrap(self.coord[other_axis] + other_delta)}
        return c["z"] * RING + c["y"]


class Link:
    def __init__(self, sems):
        self.send_sem, self.recv_sems = sems

    def make(self, src, dst, index, device):
        return pltpu.make_async_remote_copy(src_ref=src, dst_ref=dst, send_sem=self.send_sem, recv_sem=self.recv_sems.at[index],
                                            device_id=device, device_id_type=MESH)

    def go(self, src, dst, index, device):
        self.make(src, dst, index, device).start()

    def wait(self, ref, index, device):
        self.make(ref, ref, index, device).wait_recv()

    def done(self):
        ref = self.sent()
        self.make(ref, ref, 0, self.place.peer("x", 1)).wait_send()


def enter(devices):
    barrier = pltpu.get_barrier_semaphore()
    for device in devices:
        pl.semaphore_signal(barrier, inc=1, device_id=device, device_id_type=MESH)
    pl.semaphore_wait(barrier, len(devices))


def tx_devices(place):
    return [{"tx": wrap(place.tx + d, TX)} for d in range(1, TX)]


class Exchange(Link):
    def __init__(self, place, piece, out, sems):
        super().__init__(sems)
        self.place, self.piece, self.out = place, piece, out

    def target(self, i):
        return self.out.at[i]

    def send(self):
        place = self.place
        for dx in ORDER:
            for flip in BOTH:
                if dx or flip:
                    to = wrap(place.coord["x"] + dx) * 2 + (1 - place.core if flip else place.core)
                    self.go(self.piece(to), self.target(place.tx), 0, {"tx": to})

    def sent(self):
        return self.out.at[pl.ds(0, self.out.shape[0] - 1)]

    def own(self):
        self.target(self.place.tx)[...] = self.piece(self.place.tx)[...]

    def recv(self):
        self.wait(self.sent(), 0, self.place.sibling)


class TyGather(Link):
    def __init__(self, place, buf, sems):
        super().__init__(sems)
        self.place, self.buf = place, buf
        self.rows = buf.shape[0] // TY

    def message(self, half, phase, d, kind, receiving):
        place = self.place
        first, second = ("z", "y") if half == 0 else ("y", "z")
        axis = second if phase else first
        side = 1 - 2 * (kind % 2)
        hops = (0, 0, -1, 1)[kind]
        if receiving:
            hops = hops - side
        slot = place.slot(first, d, second, hops) if phase else place.slot(first, hops, second, 0)
        q = self.rows // 4
        start = slot * self.rows + 2 * q * half + (q if kind == 3 else 0)
        ref = self.buf.at[aligned(start, 2 * q if kind < 2 else q)]
        number = kind + (0 if not phase else 4 + 2 * d if kind < 2 else 10)
        return ref, half * 14 + number, place.peer(axis, side)

    def send(self, half, phase, d, kinds=BOTH):
        for kind in kinds:
            ref, index, device = self.message(half, phase, d, kind, False)
            self.go(ref, ref, index, device)

    def recv(self, half, phase, d, kind):
        self.wait(*self.message(half, phase, d, kind, True))

    def sent(self):
        return self.buf.at[pl.ds(0, (TY - 1) * self.rows)]

    def start(self):
        for phase in BOTH:
            for half in BOTH:
                self.send(half, phase, 0)

    def relay(self, half, phase, d):
        for kind in BOTH:
            self.recv(half, phase, d, kind)
            self.send(half, phase, d, (2 + kind,))

    def opposite(self, half, phase, d):
        for kind in BOTH:
            self.recv(half, phase, d, 2 + kind)

    def step_first(self):
        for half in BOTH:
            self.relay(half, 0, 0)
        for half in BOTH:
            self.send(half, 1, 3)
            self.send(half, 1, 1)

    def step_second(self):
        for half in BOTH:
            self.opposite(half, 0, 0)
            self.send(half, 1, 2)

    def step_forward(self, d):
        for half in BOTH:
            self.relay(half, 1, d)

    def finish(self):
        for half in BOTH:
            for kind in (2, 3):
                _, index, device = self.message(half, 1, 0, kind, True)
                self.wait(self.buf.at[pl.ds(0, self.rows)], index, device)


class TyScatter(Link):
    def __init__(self, place, x, got, made, mid, out, sems):
        super().__init__(sems)
        self.place, self.x, self.got, self.made, self.mid, self.out = place, x, got, made, mid, out
        self.rows = out.shape[0]
        self.q = self.rows // 4

    def axes(self, half, phase):
        return ("z", "y") if half != phase else ("y", "z")

    def part(self, half, phase, d, c, quarter):
        big, small = self.axes(half, 0)
        if phase:
            return self.mid.at[half, c, pl.ds(self.q * quarter, self.q)]
        start = self.place.slot(big, c, small, d) * self.rows + self.q * (2 * half + quarter)
        return self.x.at[aligned(start, self.q)]

    def number(self, half, phase, d):
        return half * 5 + (4 if phase else d)

    def send(self, half, phase, d, kinds=BOTH):
        n = self.number(half, phase, d)
        for kind in kinds:
            if kind < 4:
                c, quarter = ((2, 0), (2, 1), (1, 1), (3, 0))[kind]
                src = self.part(half, phase, d, c, quarter)
            else:
                src = self.made.at[n * 2 + kind - 4]
            self.go(src, self.got.at[n * 6 + kind], self.semaphore(half, phase, d, kind), self.place.peer(self.axes(half, phase)[0], 1 - 2 * (kind % 2)))

    def semaphore(self, half, phase, d, kind):
        if phase:
            return half * 24 + 18 + kind
        return half * 24 + (14 + kind if kind in (2, 3) else 4 * d + kind % 4 + kind // 4 * 2)

    def recv(self, half, phase, d, kind):
        ref = self.got.at[self.number(half, phase, d) * 6 + kind]
        if phase or kind not in (2, 3):
            self.wait(ref, self.semaphore(half, phase, d, kind), self.place.sibling)
        return ref[...].astype(F32)

    def directs(self):
        for half in BOTH:
            for kind in (2, 3):
                self.wait(self.x.at[pl.ds(0, self.rows)], self.semaphore(half, 0, 0, kind), self.place.sibling)

    def relay(self, half, phase, d):
        n = self.number(half, phase, d)
        for kind in BOTH:
            theirs = self.part(half, phase, d, 1 + 2 * kind, kind)[...].astype(F32)
            self.made[n * 2 + kind] = (self.recv(half, phase, d, kind) + theirs).astype(BF16)
            self.send(half, phase, d, (4 + kind,))

    def total(self, half, phase, d, quarter):
        value = self.part(half, phase, d, 0, quarter)[...].astype(F32)
        value = value + self.recv(half, phase, d, 3 - quarter)
        return value + self.recv(half, phase, d, 4 + quarter)

    def sent(self):
        return self.x.at[pl.ds(0, (TY - 1) * self.rows)]

    def start(self, halves=BOTH):
        for kinds in (BOTH, (2, 3)):
            for d in ORDER:
                for half in halves:
                    self.send(half, 0, d, kinds)

    def fill(self, compute):
        def body(t, carry):
            d = wrap(t + 2)
            compute(wrap(self.place.coord["z"] + d))
            self.send(0, 0, d, range(4))
            return carry

        lax.fori_loop(0, RING, body, 0)
        self.start((1,))

    def relays(self, *ds):
        for d in ds:
            for half in BOTH:
                self.relay(half, 0, d)

    def middle(self, *ds):
        if ds[0] == ORDER[0]:
            self.directs()
        for d in ds:
            for half in BOTH:
                for quarter in BOTH:
                    value = self.total(half, 0, d, quarter)
                    self.mid[half, d, pl.ds(self.q * quarter, self.q)] = value.astype(BF16)
                if d:
                    self.send(half, 1, 0, {2: BOTH, 3: (3,), 1: (2,)}[d])

    def last_relay(self):
        for half in BOTH:
            self.relay(half, 1, 0)

    def finish(self):
        for half in BOTH:
            for quarter in BOTH:
                self.out[pl.ds(self.q * (2 * half + quarter), self.q)] = self.total(half, 1, 0, quarter)


SCATTER_SEMS = 60


def scatter_scratch(rows, width):
    q = rows // 4
    return [pltpu.VMEM((SCATTER_SEMS, q, width), BF16), pltpu.VMEM((20, q, width), BF16),
            pltpu.VMEM((2, 4, 2 * q, width), BF16), pltpu.VMEM((rows, width), F32)]


SEMS = dict(h=1, r=1, g=1, s=1, e=1, q=1, d=1, o=1, ty=1, gate=10, up=5, down=10, proj=10, ag1=28, rs1=48, rs2=48, pair=RING,
            local=13, send=22)


class TxGather(Link):
    def __init__(self, place, own, view, sems):
        super().__init__(sems)
        self.place, self.own_ref, (self.view, self.blocks) = place, own, view
        self.rows = own.shape[0]

    def ref(self, delta, part=None):
        owner = wrap(self.place.coord["x"] + delta) * 2 + self.place.core
        half = self.rows // 2
        return self.view(owner, 0, self.rows) if part is None else self.view(owner, part * half, half)

    def sent(self):
        return self.blocks(TX - 1)

    def start(self):
        for kind, side in SIDES:
            self.go(self.own_ref, self.ref(0), kind, self.place.peer("x", side))
        self.go(self.own_ref, self.ref(0), 4, self.place.sibling)

    def share(self, delta):
        self.go(self.ref(delta), self.ref(delta), 4, self.place.sibling)

    def forward(self):
        for kind, side in SIDES:
            self.wait(self.ref(-side), kind, self.place.peer("x", side))
            part = self.ref(-side, kind)
            self.go(part, part, 2 + kind, self.place.peer("x", side))
            self.share(-side)

    def last(self):
        for kind, side in SIDES:
            self.wait(self.ref(2, kind), 2 + kind, self.place.peer("x", side))
        self.share(2)

    def finish(self):
        self.wait(self.blocks(RING), 4, self.place.sibling)


def row_view(ref, block, columns):
    return (lambda owner, start, rows: ref.at[aligned(owner * block + start, rows), columns],
            lambda n: ref.at[pl.ds(0, n * block), columns])


def column_view(ref, width):
    return (lambda owner, start, rows: ref.at[pl.ds(start, rows), chunk(owner, width)],
            lambda n: ref.at[:, pl.ds(0, n * width)])


class Local:
    def __init__(self, sem):
        self.sem = sem
        self.copies = []

    def go(self, src, dst):
        copy = pltpu.make_async_copy(src, dst, self.sem.at[len(self.copies)])
        copy.start()
        self.copies.append(copy)
        return copy


def swap_rows(value):
    size = value.shape[0]
    row = lax.broadcasted_iota(jnp.int32, (size, size), 0)
    col = lax.broadcasted_iota(jnp.int32, (size, size), 1)
    swap = jnp.where(row == col + 1 - 2 * lax.rem(col, 2), 1.0, 0.0).astype(BF16)
    return dot(swap, value, NN)


def rotated(value, cos_t, sin_t):
    return value.astype(F32) * cos_t + swap_rows(value) * sin_t


def join_halves(left, right, swap_left):
    half = left.shape[1] // 2
    lane = lax.broadcasted_iota(jnp.int32, left.shape, 1)
    if swap_left:
        left = pltpu.roll(left, half, 1)
    else:
        right = pltpu.roll(right, half, 1)
    return jnp.where(lane < half, left, right)


def column(i, width):
    return slice(i * width, (i + 1) * width)


class TxScatter(Link):
    def __init__(self, place, piece, give, paired, got, made, out, sems, pair_sems):
        super().__init__(sems)
        self.pair_sems = pair_sems
        self.place, self.piece, self.give, self.paired, self.summed = place, piece, give, paired, give
        self.got, self.made, self.out = got, made, out
        self.half = out.shape[0] // 2

    def owner(self, d, core):
        return wrap(self.place.coord["x"] + d) * 2 + core

    def handover(self, d):
        return pltpu.make_async_remote_copy(
            src_ref=self.give.at[d], dst_ref=self.paired.at[d], send_sem=self.pair_sems.at[d],
            recv_sem=self.recv_sems.at[6 + d], device_id=self.place.sibling, device_id_type=MESH)

    def sent(self):
        return self.got

    def start(self):
        def body(t, carry):
            d = wrap(t + 2)
            self.give[d] = self.piece(self.owner(d, 1 - self.place.core)).astype(BF16)
            self.handover(d).start()
            return carry

        lax.fori_loop(0, RING, body, 0)

    def pair(self):
        def body(t, carry):
            d = wrap(t + 2)
            value = self.piece(self.owner(d, self.place.core))
            self.handover(d).wait()
            self.summed[d] = (value + self.paired[d].astype(F32)).astype(BF16)
            return carry

        lax.fori_loop(0, RING, body, 0)
        self.ring(range(4))

    def ring(self, kinds):
        for kind in kinds:
            if kind < 4:
                d, part = ((2, 0), (2, 1), (1, 1), (3, 0))[kind]
                src = self.summed.at[d, pl.ds(part * self.half, self.half)]
            else:
                src = self.made.at[kind - 4]
            self.go(src, self.got.at[kind], kind, self.place.peer("x", 1 - 2 * (kind % 2)))

    def each(self, step, count, body):
        def run(k, carry):
            body(k * step)
            return carry

        lax.fori_loop(0, count // step, run, 0)

    def relay(self):
        for kind in BOTH:
            self.wait(self.got.at[kind], kind, self.place.peer("x", 1))

            def body(start, kind=kind):
                rows = aligned(start, 32, 32)
                theirs = self.summed[1 + 2 * kind, aligned(kind * self.half + start, 32, 32)]
                self.made[kind, rows] = (self.got[kind, rows].astype(F32) + theirs.astype(F32)).astype(BF16)

            self.each(32, self.half, body)
            self.ring((4 + kind,))

    def finish(self):
        for part in BOTH:
            for kind in (3 - part, 4 + part):
                self.wait(self.got.at[kind], kind, self.place.peer("x", 1))

            def body(start, part=part):
                rows = aligned(start, 32, 32)
                full = aligned(part * self.half + start, 32, 32)
                value = self.summed[0, full].astype(F32) + self.got[3 - part, rows].astype(F32)
                self.out[full] = value + self.got[4 + part, rows].astype(F32)

            self.each(32, self.half, body)


def tx_scratch(rows, width):
    full = pltpu.VMEM((RING, rows, width), BF16)
    return [full, full, pltpu.VMEM((6, rows // 2, width), BF16), pltpu.VMEM((2, rows // 2, width), BF16)]


def main_kernel(dh2, wg, wu, wd, wq, wkv, *rest):
    inputs, outputs, entered, rest = rest[:7], rest[7:15], rest[15:22], rest[22:]
    h, dq, dkv, positions, freq, g_ffn, g_attn = entered
    resid, dh, q_out, kv_out, dgu, dwd, dproj, dg_out = outputs
    (n_all, wgu, wd_all, wqkv_all, ab, u, eq_t, e_all, x1, x2, eq_send, qkv_r, wqkv, h_t, h2_t, dh2_t, dh_t, dres_t,
     g_all, dg_part, dg_x, dg_y, cos_t, sin_t) = rest[:24]
    rest = rest[24:]
    place = Place()
    rs_scratch1, rs_scratch2 = rest[:4], rest[4:8]
    tx_refs = [rest[8 + 4 * k:12 + 4 * k] for k in range(3)]
    recv, recv_names = rest[20:], list(SEMS)
    local = Local(recv[recv_names.index("local")])
    n2_all, x3, qkv_send, gains = x1, x2, eq_send, dg_y.at[0]
    width = h.shape[2]
    model_dim = TX * width
    ffn = wg.shape[1]
    nq = dq.shape[0]
    head = cos_t.shape[0]
    tile = eq_send.shape[2]
    used = []

    def sems(name):
        used.append(name)
        return recv[recv_names.index("send")].at[len(used) - 1], recv[recv_names.index(name)]

    pair_sems = recv[recv_names.index("pair")]
    ex_h = Exchange(place, lambda i: h.at[i], h_t, sems("h"))
    ex_r = Exchange(place, lambda i: h2_t.at[i], resid, sems("r"))
    ex_g = Exchange(place, lambda i: gains, g_all, sems("g"))
    ex_s = Exchange(place, lambda i: dg_part.at[i], dg_x, sems("s"))
    ex_e = Exchange(place, lambda i: eq_send.at[i], eq_send, sems("e"))
    ex_e.target = lambda i: eq_t.at[:, chunk(i, tile)]
    ex_q = Exchange(place, lambda i: qkv_send.at[i], qkv_r, sems("q"))
    ex_d = Exchange(place, lambda i: dh2.at[i], dh2_t, sems("d"))
    ex_o = Exchange(place, lambda i: dh_t.at[i], dh, sems("o"))
    w_gate = TxGather(place, wg, row_view(wgu, width, pl.ds(0, ffn)), sems("gate"))
    w_up = TxGather(place, wu, row_view(wgu, width, pl.ds(ffn, ffn)), sems("up"))
    w_down = TxGather(place, wd, column_view(wd_all, width), sems("down"))
    w_proj = TxGather(place, wqkv, column_view(wqkv_all, width), sems("proj"))
    down_grad = TxScatter(place, lambda i: dot(u[...], e_all[:, chunk(i, width)], TN), *tx_refs[0], dwd, sems("down"), pair_sems)
    gate_grad = TxScatter(place, lambda i: dot(n_all[:, chunk(i, width)], ab[...], TN), *tx_refs[1], dgu, sems("gate"), pair_sems)
    proj_grad = TxScatter(place, lambda i: dot(eq_t[...], n2_all[:, chunk(i, width)], NN), *tx_refs[2], dproj, sems("proj"),
                          pair_sems)
    gain_link = Exchange(place, None, dg_y, sems("ty"))
    gather = TyGather(place, n_all, sems("ag1"))
    ag_e = TyGather(place, e_all, sems("ag1"))
    ag_n = TyGather(place, n2_all, sems("rs1"))
    rs1 = TyScatter(place, x1, *rs_scratch1, sems("rs1"))
    rs2 = TyScatter(place, x2, *rs_scratch2, sems("rs2"))
    rs3 = TyScatter(place, x3, *rs_scratch2, sems("rs2"))
    entries = [local.go(src, dst) for src, dst in zip(inputs, entered)]
    entries += [local.go(wq, wqkv.at[pl.ds(0, nq)]), local.go(wkv, wqkv.at[pl.ds(nq, wkv.shape[0])])]
    enter(tx_devices(place) + [place.peer(axis, d) for axis in ("z", "y") for d in (1, -1)])
    for copy in entries:
        copy.wait()
    gains[0:1] = g_ffn[...].astype(F32).reshape(1, width)
    gains[1:2] = g_attn[...].astype(F32).reshape(1, width)
    ex_g.send()
    ex_h.send()
    own_copies = [local.go(w.own_ref, w.ref(0)) for w in (w_gate, w_up, w_down)]
    own_copies.append(local.go(dh2.at[place.tx], dh2_t.at[place.tx]))
    angles = freq[...] * positions[...].astype(F32)
    odd_row = lax.rem(lax.broadcasted_iota(jnp.int32, angles.shape, 0), 2) == 1
    cos_t[...] = jnp.cos(angles)
    sine = jnp.sin(angles)
    sin_t[...] = jnp.where(odd_row, sine, -sine)
    turned = place.ty < TY // 2
    for base, ref in ((0, dq), (nq, dkv)):
        for k in range(ref.shape[0] // head):
            rows = slice(k * head, (k + 1) * head)
            out_rows = slice(base + k * head, base + (k + 1) * head)
            value = rotated(ref[rows], cos_t[...], -sin_t[...])
            if base:
                value = jnp.where(turned, value, ref[rows].astype(F32))
            for m in range(TX // 2):
                near, far = value[:, column(m, tile)], value[:, column(m + TX // 2, tile)]
                for odd in BOTH:
                    eq_send[2 * m + odd, out_rows] = join_halves(near, far, odd).astype(BF16)
    ex_e.send()
    w_proj.start()
    w_gate.start()
    ex_e.own()
    w_proj.ref(0)[...] = wqkv[...]
    ex_h.own()
    ex_g.own()
    ex_h.recv()
    ex_g.recv()
    ex_g.done()
    mine = aligned(place.ty * gather.rows, gather.rows)

    def inverse_rms(ref):
        squares = 0.0
        for i in range(TX):
            x = ref[i].astype(F32)
            squares = squares + jnp.sum(x * x, axis=1, keepdims=True)
        return lax.rsqrt(squares / model_dim + NORM_EPS)

    inv1 = inverse_rms(h_t)
    for i in range(TX):
        n_all[mine, column(i, width)] = (h_t[i].astype(F32) * inv1 * g_all[i, 0:1]).astype(BF16)
    gather.start()
    gather.step_first()
    w_proj.forward()
    w_up.start()
    ex_e.recv()
    gather.step_second()
    w_gate.forward()
    w_proj.last()
    gather.step_forward(0)
    w_proj.finish()

    def back_projection(k, carry):
        x2[chunk(k, 256)] = dot(eq_t[:, chunk(k, 256)], wqkv_all[...], TN).astype(BF16)
        return carry

    lax.fori_loop(0, 4, back_projection, 0)
    gather.step_forward(3)
    gather.step_forward(1)
    w_up.forward()
    w_down.start()
    gather.step_forward(2)
    rs2.start()
    w_gate.last()
    gather.finish()
    for copy in own_copies:
        copy.wait()
    w_up.last()
    w_gate.finish()
    w_up.finish()

    def gate_up(k, carry):
        rows = chunk(k, 256)
        both = dot(n_all[rows], wgu[...], NN).astype(BF16)
        ab[rows] = both
        gate = both[:, :ffn].astype(F32)
        u[rows] = (gate * jax.nn.sigmoid(gate) * both[:, ffn:].astype(F32)).astype(BF16)
        return carry

    def down(k):
        x1[chunk(k, 256)] = dot(u[chunk(k, 256)], wd_all[...], NN).astype(BF16)

    lax.fori_loop(0, 2, gate_up, 0)
    w_down.forward()
    ex_d.send()
    rs2.relays(*ORDER)
    lax.fori_loop(2, 4, gate_up, 0)
    w_down.last()
    w_down.finish()
    rs1.fill(down)
    rs2.middle(*ORDER)
    rs1.relays(*ORDER)
    rs2.last_relay()
    rs1.middle(2, 3, 1)
    rs2.finish()
    ex_d.recv()
    rs1.middle(0)
    rs1.last_relay()
    rs2.done()
    rs1.finish()
    for i in range(TX):
        h2_t[i] = (h_t[i].astype(F32) + rs1.out[:, column(i, width)]).astype(BF16)
    inv2 = inverse_rms(h2_t)
    inner = 0.0
    for i in range(TX):
        x = h2_t[i].astype(F32)
        grad = rs2.out[:, column(i, width)]
        dg_part[i, 1:2] = jnp.sum(grad * x * inv2, axis=0, keepdims=True)
        inner = inner + jnp.sum(grad * g_all[i, 1:2] * x, axis=1, keepdims=True)
    cubed = inv2 * inv2 * inv2 * (inner / model_dim)
    for i in range(TX):
        grad = rs2.out[:, column(i, width)] * g_all[i, 1:2]
        value = dh2_t[i].astype(F32) + (inv2 * grad - h2_t[i].astype(F32) * cubed)
        dres_t[i] = value
        e_all[mine, column(i, width)] = value.astype(BF16)
    rs1.done()
    ag_e.start()
    for i in range(TX):
        n2_all[mine, column(i, width)] = (h2_t[i].astype(F32) * inv2 * g_all[i, 1:2]).astype(BF16)
    ex_r.send()
    ex_r.own()
    ag_e.step_first()
    ag_e.step_second()
    for d in SPREAD:
        ag_e.step_forward(d)
    ag_n.start()
    ag_e.finish()

    def grad_act(k, carry):
        rows = chunk(k, 256)
        grad = dot(e_all[rows], wd_all[...], NT)
        gate = ab[rows, :ffn].astype(F32)
        up = ab[rows, ffn:].astype(F32)
        sig = jax.nn.sigmoid(gate)
        ab[rows, :ffn] = (grad * up * sig * (1.0 + gate * (1.0 - sig))).astype(BF16)
        ab[rows, ffn:] = (grad * gate * sig).astype(BF16)
        return carry

    def grad_norm(k):
        x3[chunk(k, 256)] = dot(ab[chunk(k, 256)], wgu[...], NT).astype(BF16)

    def project(k, carry):
        value = dot(wqkv_all[...], n2_all[chunk(k, 256)], NT).astype(BF16)
        qkv_send[2 * k] = value[:, :tile]
        qkv_send[2 * k + 1] = value[:, tile:]
        return carry

    ex_r.recv()
    down_grad.start()
    ag_n.step_first()
    down_grad.pair()
    lax.fori_loop(0, 4, grad_act, 0)
    ag_n.step_second()
    gate_grad.start()
    down_grad.relay()
    ag_n.step_forward(0)
    gate_grad.pair()
    ag_n.step_forward(3)
    ag_n.step_forward(1)
    ag_n.step_forward(2)
    rs3.fill(grad_norm)
    down_grad.finish()
    gate_grad.relay()
    ag_n.finish()
    ex_e.done()
    lax.fori_loop(0, 4, project, 0)
    ex_q.send()
    ex_q.own()
    proj_grad.start()
    rs3.relays(*ORDER)
    proj_grad.pair()
    rs3.middle(*ORDER)
    gate_grad.finish()
    rs3.last_relay()
    proj_grad.relay()
    rs3.finish()
    inner = 0.0
    for i in range(TX):
        x = h_t[i].astype(F32)
        grad = rs3.out[:, column(i, width)]
        dg_part[i, 0:1] = jnp.sum(grad * x * inv1, axis=0, keepdims=True)
        inner = inner + jnp.sum(grad * g_all[i, 0:1] * x, axis=1, keepdims=True)
    ex_s.send()
    ex_s.own()
    cubed = inv1 * inv1 * inv1 * (inner / model_dim)
    for i in range(TX):
        grad = rs3.out[:, column(i, width)] * g_all[i, 0:1]
        dh_t[i] = (dres_t[i] + (inv1 * grad - h_t[i].astype(F32) * cubed)).astype(BF16)
    ex_o.send()
    ex_o.own()
    ex_q.recv()
    for m in range(TX):
        even = 2 * (m % RING)
        cols = column(m, tile)
        left, right = qkv_r[even].astype(F32), qkv_r[even + 1].astype(F32)
        value = join_halves(left, right, m >= RING).astype(BF16)
        for k in range(nq // head):
            q_out[column(k, head), cols] = rotated(value[column(k, head)], cos_t[:, cols], sin_t[:, cols]).astype(BF16)
        for k in range(kv_out.shape[0] // head):
            part = value[nq + k * head:nq + (k + 1) * head]
            spun = rotated(part, cos_t[:, cols], sin_t[:, cols])
            kv_out[column(k, head), cols] = jnp.where(turned, spun, part.astype(F32)).astype(BF16)
    ex_s.recv()
    total = dg_x[0]
    for i in range(1, TX):
        total = total + dg_x[i]
    dg_y[place.ty] = total
    for d in range(1, TY):
        gain_link.go(dg_y.at[place.ty], dg_y.at[place.ty], 0, {"ty": wrap(place.ty + d, TY)})
    proj_grad.finish()
    ex_o.recv()
    gain_link.recv()
    total = dg_y[0]
    for j in range(1, TY):
        total = total + dg_y[j]
    dg_out[0] = total[0:1]
    dg_out[1] = total[1:2]
    for item in (ex_h, ex_d, ex_r, ex_q, ex_o, ex_s, gather, w_gate, w_up, w_down, w_proj,
                 ag_e, ag_n, rs3, gain_link, down_grad, gate_grad, proj_grad):
        item.done()


def store_kernel(resid, dh, q_t, kv_t, dgu, dwd, dproj, dg,
                 resid_o, dh_o, q_o, kv_o, dga_o, dgb_o, dwg_o, dwu_o, dwd_o, dwq_o, dwkv_o, sems):
    ffn = dwg_o.shape[1]
    nq, nkv = q_o.shape[0], kv_o.shape[0]
    moves = [(dgu.at[:, pl.ds(0, ffn)], dwg_o), (dgu.at[:, pl.ds(ffn, ffn)], dwu_o), (dwd, dwd_o), (resid, resid_o), (dh, dh_o),
             (q_t, q_o), (kv_t, kv_o), (dproj.at[pl.ds(0, nq)], dwq_o), (dproj.at[pl.ds(nq, nkv)], dwkv_o),
             (dg.at[0], dga_o), (dg.at[1], dgb_o)]
    stores = [pltpu.make_async_copy(src, dst, sems.at[k]) for k, (src, dst) in enumerate(moves)]
    for copy in stores:
        copy.start()
    for copy in stores:
        copy.wait()


HBM_SPEC = pl.BlockSpec(memory_space=pl.ANY)


VMEM_SPEC = pl.BlockSpec(memory_space=pltpu.VMEM)


def call(kernel, number, ins, outs, scratch):
    in_spec, out_spec = (HBM_SPEC, VMEM_SPEC) if number is not None else (VMEM_SPEC, HBM_SPEC)
    shape_of = pltpu.VMEM if number is not None else jax.ShapeDtypeStruct
    return pl.pallas_call(
        kernel, out_shape=[shape_of(shape, dtype) for shape, dtype in outs],
        in_specs=[in_spec] * len(ins), out_specs=[out_spec] * len(outs), scratch_shapes=scratch,
        compiler_params=pltpu.CompilerParams(collective_id=number, has_side_effects=number is not None,
                                             vmem_limit_bytes=(59 if number is not None else 4) * 2 ** 20),
        name=kernel.__name__)(*ins)


def solution(mesh):
    def local_step(hidden, positions, g_ffn, w_gate, w_up, w_down, g_attn, w_q, w_kv, grad_h2, grad_q, grad_kv):
        rows, width = hidden.shape
        model_dim = width * TX
        ffn = w_gate.shape[1]
        head_dim = w_q.shape[2]
        tokens = positions.shape[0]

        def features(value):
            return value.transpose(1, 2, 0).reshape(-1, value.shape[0])

        def unfeatures(value):
            return value.reshape(-1, head_dim, value.shape[1]).transpose(2, 0, 1)

        dq, dkv, wq, wkv = features(grad_q), features(grad_kv), features(w_q), features(w_kv)
        nq = dq.shape[0]
        proj = nq + dkv.shape[0]
        own = rows // TX
        inv_freq = ROPE_BASE ** (-np.arange(0, head_dim, 2) / head_dim)
        freq = np.repeat(inv_freq, 2).astype(np.float32)[:, None]
        own = (own, model_dim)
        whole = (tokens, model_dim)
        piece = (TX, own[0], width)
        tile = tokens // TX
        wide = (TX, proj, tile)
        flat = (rows, width)
        gain = (TX, 2, width)
        vmem = [(whole, BF16), ((model_dim, 2 * ffn), BF16), ((ffn, model_dim), BF16), ((proj, model_dim), BF16),
                ((tokens, 2 * ffn), BF16), ((tokens, ffn), BF16), ((proj, tokens), BF16),
                (whole, BF16), (whole, BF16), (whole, BF16), (wide, BF16), (wide, BF16), ((proj, width), BF16),
                (piece, BF16), (piece, BF16), (piece, BF16), (piece, BF16), (piece, F32), (gain, F32), (gain, F32), (gain, F32),
                ((TY, 2, width), F32), ((head_dim, tokens), F32), ((head_dim, tokens), F32)]
        results = [(piece, BF16), (piece, BF16), ((nq, tokens), BF16), ((proj - nq, tokens), BF16),
                   ((width, 2 * ffn), F32), ((ffn, width), F32), ((proj, width), F32), ((2, 1, width), F32)]
        entering = (hidden.reshape(piece), dq, dkv, positions.reshape(1, tokens), freq, g_ffn, g_attn)
        outs = call(
            main_kernel, 0,
            [grad_h2.reshape(piece), w_gate, w_up, w_down, wq, wkv, *entering],
            results,
            [pltpu.VMEM(value.shape, value.dtype) for value in entering] + [pltpu.VMEM(shape, dtype) for shape, dtype in vmem]
            + scatter_scratch(*own) * 2 + tx_scratch(ffn, width) + tx_scratch(width, 2 * ffn) + tx_scratch(proj, width)
            + [pltpu.SemaphoreType.DMA((n,)) for n in SEMS.values()])
        gains_out = ((1, width), F32)
        resid, dh, q_t, kv_t, dga, dgb, dwg, dwu, dwd, dwq, dwkv = call(
            store_kernel, None,
            [pltpu.with_memory_space_constraint(value, pltpu.VMEM) for value in outs],
            results[:4] + [gains_out] * 2
            + [((width, ffn), F32), ((width, ffn), F32), ((ffn, width), F32), ((nq, width), F32), ((proj - nq, width), F32)],
            [pltpu.SemaphoreType.DMA((TY,))])
        return (resid.reshape(flat), unfeatures(q_t), unfeatures(kv_t), dh.reshape(flat), dga[0], dgb[0],
                dwg, dwu, dwd, unfeatures(dwq), unfeatures(dwkv))

    row_spec = P(("dp", "ty"), "tx")
    head_spec = P(("dp", "tx"), "ty", None)
    in_specs = (row_spec, P(("dp", "tx")), P("tx"), P("tx", "ty"), P("tx", "ty"), P("ty", "tx"), P("tx"), P("tx", "ty", None), P("tx", "ty", None), row_spec, head_spec, head_spec)
    out_specs = (row_spec, head_spec, head_spec, row_spec, P(("dp", "tx")), P(("dp", "tx")), P(("dp", "tx"), "ty"), P(("dp", "tx"), "ty"), P(("dp", "ty"), "tx"), head_spec, head_spec)
    return jax.shard_map(local_step, mesh=mesh, in_specs=in_specs, out_specs=out_specs, check_vma=False)
```

profile of v0, /device:TPU:1, one launch (start us, length us, event | category | flops | bytes accessed | tf_op | source)
XLA Modules:
  0.0 164.5 jit_solution(17670052741828566576)
XLA Ops:
  0.6 162.2 %main_kernel.1 = (bf16[8,64,256]{2,1,0:T(8,128)(2,1)S(1)}, bf16[8,64,256]{2,1,0:T(8,128)(2,1)S(1)}, bf16[128,1024]{1,0:T(8,128)(2,1)S(1)}, bf16[64,1024]{1,0:T(8...) custom-call(bf16[8,64,256]{2,1,0:T(8,128)(2,1)} %bitcast.31, ...), custom_call_target="tpu_custom_call" | custom-call | tf_op jit(solution)/shard_map/main_kernel/pallas_call | solution.py:780
  162.9 1.6 store_kernel.1
where the time goes:
time: 165 us; the launch traced here: 164 us
  Pallas kernels  164 us (99%)
    pallas_call x2, Pallas kernels, call(): pl.pallas_call(kernel, out_shape=[shape_of(shape, dtype) for shape, dtype...  164 us

commit v1 on v0

--- a/solution.py
+++ b/solution.py
@@ -19,6 +19,7 @@
 ORDER = (2, 3, 1, 0)
 SPREAD = (0, 3, 1, 2)
 BOTH = (0, 1)
+DIRECT = {2: BOTH, 3: (3,), 1: (2,), 0: ()}
 SIDES = ((0, 1), (1, -1))
 MESH = pl.DeviceIdType.MESH
 
@@ -127,15 +128,17 @@
         first, second = ("z", "y") if half == 0 else ("y", "z")
         axis = second if phase else first
         side = 1 - 2 * (kind % 2)
-        hops = (0, 0, -1, 1)[kind]
+        hops = (0, 0, -1, 1, 0, 0)[kind]
         if receiving:
             hops = hops - side
         slot = place.slot(first, d, second, hops) if phase else place.slot(first, hops, second, 0)
         q = self.rows // 4
-        start = slot * self.rows + 2 * q * half + (q if kind == 3 else 0)
-        ref = self.buf.at[aligned(start, 2 * q if kind < 2 else q)]
-        number = kind + (0 if not phase else 4 + 2 * d if kind < 2 else 10)
-        return ref, half * 14 + number, place.peer(axis, side)
+        start = slot * self.rows + 2 * q * half
+        if not phase or kind > 1:
+            start = start + q * (kind % 2 if kind < 4 else 5 - kind)
+        ref = self.buf.at[aligned(start, 2 * q if phase and kind < 2 else q)]
+        number = kind + (0 if not phase else 6 + 2 * d if kind < 2 else 12)
+        return ref, half * TY + number, place.peer(axis, side)
 
     def send(self, half, phase, d, kinds=BOTH):
         for kind in kinds:
@@ -149,9 +152,10 @@
         return self.buf.at[pl.ds(0, (TY - 1) * self.rows)]
 
     def start(self):
-        for phase in BOTH:
-            for half in BOTH:
-                self.send(half, phase, 0)
+        for half in BOTH:
+            self.send(half, 0, 0, (0, 1, 5, 4))
+        for half in BOTH:
+            self.send(half, 1, 0)
 
     def relay(self, half, phase, d):
         for kind in BOTH:
@@ -166,7 +170,9 @@
         for half in BOTH:
             self.relay(half, 0, 0)
         for half in BOTH:
+            self.recv(half, 0, 0, 4)
             self.send(half, 1, 3)
+            self.recv(half, 0, 0, 5)
             self.send(half, 1, 1)
 
     def step_second(self):
@@ -246,21 +252,18 @@
     def sent(self):
         return self.x.at[pl.ds(0, (TY - 1) * self.rows)]
 
-    def start(self, halves=BOTH):
+    def start(self):
         for kinds in (BOTH, (2, 3)):
             for d in ORDER:
-                for half in halves:
+                for half in BOTH:
                     self.send(half, 0, d, kinds)
 
     def fill(self, compute):
-        def body(t, carry):
-            d = wrap(t + 2)
+        for d in ORDER:
             compute(wrap(self.place.coord["z"] + d))
             self.send(0, 0, d, range(4))
-            return carry
-
-        lax.fori_loop(0, RING, body, 0)
-        self.start((1,))
+            for piece in ORDER:
+                self.send(1, 0, piece, DIRECT[d])
 
     def relays(self, *ds):
         for d in ds:
@@ -275,8 +278,7 @@
                 for quarter in BOTH:
                     value = self.total(half, 0, d, quarter)
                     self.mid[half, d, pl.ds(self.q * quarter, self.q)] = value.astype(BF16)
-                if d:
-                    self.send(half, 1, 0, {2: BOTH, 3: (3,), 1: (2,)}[d])
+                self.send(half, 1, 0, DIRECT[d])
 
     def last_relay(self):
         for half in BOTH:
@@ -297,7 +299,7 @@
             pltpu.VMEM((2, 4, 2 * q, width), BF16), pltpu.VMEM((rows, width), F32)]
 
 
-SEMS = dict(h=1, r=1, g=1, s=1, e=1, q=1, d=1, o=1, ty=1, gate=10, up=5, down=10, proj=10, ag1=28, rs1=48, rs2=48, pair=RING,
+SEMS = dict(h=1, r=1, g=1, s=1, e=1, q=1, d=1, o=1, ty=1, gate=10, up=5, down=10, proj=10, ag1=32, rs1=48, rs2=48, pair=RING,
             local=13, send=22)
 
 
@@ -688,18 +690,18 @@
     gate_grad.start()
     down_grad.relay()
     ag_n.step_forward(0)
-    gate_grad.pair()
     ag_n.step_forward(3)
     ag_n.step_forward(1)
+    gate_grad.pair()
     ag_n.step_forward(2)
     rs3.fill(grad_norm)
     down_grad.finish()
-    gate_grad.relay()
     ag_n.finish()
     ex_e.done()
     lax.fori_loop(0, 4, project, 0)
     ex_q.send()
     ex_q.own()
+    gate_grad.relay()
     proj_grad.start()
     rs3.relays(*ORDER)
     proj_grad.pair()

time: 165 us -> 162 us (0.982)
  Pallas kernels: 164 us -> 161 us
    pallas_call x2, Pallas kernels: 164 us -> 161 us  [call(): pl.pallas_call(kernel, out_shape=[shape_of(shape, dtype) for shape, dtype...]
where the time goes in v1:
time: 162 us; the launch traced here: 161 us
  Pallas kernels  161 us (99%)
    pallas_call x2, Pallas kernels, call(): pl.pallas_call(kernel, out_shape=[shape_of(shape, dtype) for shape, dtype...  161 us

profile of v1, /device:TPU:1, one launch (start us, length us, event | category | flops | bytes accessed | tf_op | source)
XLA Modules:
  0.0 161.4 jit_solution(1948305497491459734)
XLA Ops:
  0.6 159.0 %main_kernel.1 = (bf16[8,64,256]{2,1,0:T(8,128)(2,1)S(1)}, bf16[8,64,256]{2,1,0:T(8,128)(2,1)S(1)}, bf16[128,1024]{1,0:T(8,128)(2,1)S(1)}, bf16[64,1024]{1,0:T(8...) custom-call(bf16[8,64,256]{2,1,0:T(8,128)(2,1)} %bitcast.31, ...), custom_call_target="tpu_custom_call" | custom-call | tf_op jit(solution)/shard_map/main_kernel/pallas_call | solution.py:782
  159.6 1.6 %store_kernel.1 = (bf16[8,64,256]{2,1,0:T(8,128)(2,1)}, bf16[8,64,256]{2,1,0:T(8,128)(2,1)}, bf16[128,1024]{1,0:T(8,128)(2,1)}, bf16[64,1024]{1,0:T(8,128)(2,1)}...) custom-call(bf16[8,64,256]{2,1,0:T(8,128)(2,1)S(1)} %get-tuple-eleme, ...), custom_call_target="tpu_custom_call" | custom-call | tf_op jit(solution)/shard_map/store_kernel/pallas_call | solution.py:782

commit v2 on v1

--- a/solution.py
+++ b/solution.py
@@ -19,6 +19,8 @@
 ORDER = (2, 3, 1, 0)
 SPREAD = (0, 3, 1, 2)
 BOTH = (0, 1)
+LATE = (2, 3)
+ROWS = 256
 DIRECT = {2: BOTH, 3: (3,), 1: (2,), 0: ()}
 SIDES = ((0, 1), (1, -1))
 MESH = pl.DeviceIdType.MESH
@@ -186,7 +188,7 @@
 
     def finish(self):
         for half in BOTH:
-            for kind in (2, 3):
+            for kind in LATE:
                 _, index, device = self.message(half, 1, 0, kind, True)
                 self.wait(self.buf.at[pl.ds(0, self.rows)], index, device)
 
@@ -223,19 +225,21 @@
 
     def semaphore(self, half, phase, d, kind):
         if phase:
-            return half * 24 + 18 + kind
-        return half * 24 + (14 + kind if kind in (2, 3) else 4 * d + kind % 4 + kind // 4 * 2)
+            return half * 26 + 20 + kind
+        if kind in LATE:
+            return half * 26 + TY + kind - (2 if d == ORDER[0] else 0)
+        return half * 26 + 4 * d + kind % 4 + kind // 4 * 2
 
     def recv(self, half, phase, d, kind):
         ref = self.got.at[self.number(half, phase, d) * 6 + kind]
-        if phase or kind not in (2, 3):
+        if phase or kind not in LATE:
             self.wait(ref, self.semaphore(half, phase, d, kind), self.place.sibling)
         return ref[...].astype(F32)
 
-    def directs(self):
-        for half in BOTH:
-            for kind in (2, 3):
-                self.wait(self.x.at[pl.ds(0, self.rows)], self.semaphore(half, 0, 0, kind), self.place.sibling)
+    def directs(self, d, count):
+        for half in BOTH:
+            for kind in LATE:
+                self.wait(self.x.at[pl.ds(0, count * self.q)], self.semaphore(half, 0, d, kind), self.place.sibling)
 
     def relay(self, half, phase, d):
         n = self.number(half, phase, d)
@@ -253,17 +257,21 @@
         return self.x.at[pl.ds(0, (TY - 1) * self.rows)]
 
     def start(self):
-        for kinds in (BOTH, (2, 3)):
+        for kinds in (BOTH, LATE):
             for d in ORDER:
                 for half in BOTH:
                     self.send(half, 0, d, kinds)
 
-    def fill(self, compute):
+    def fill(self, compute, pieces=ORDER):
         for d in ORDER:
             compute(wrap(self.place.coord["z"] + d))
-            self.send(0, 0, d, range(4))
+            self.send(0, 0, d, range(4) if d in pieces else BOTH)
             for piece in ORDER:
-                self.send(1, 0, piece, DIRECT[d])
+                self.send(1, 0, piece, DIRECT[d] if d == ORDER[0] or piece in pieces else ())
+
+    def direct(self, d):
+        for half in BOTH:
+            self.send(half, 0, d, LATE)
 
     def relays(self, *ds):
         for d in ds:
@@ -271,9 +279,9 @@
                 self.relay(half, 0, d)
 
     def middle(self, *ds):
-        if ds[0] == ORDER[0]:
-            self.directs()
         for d in ds:
+            if d in LATE:
+                self.directs(d, 1 if d == ORDER[0] else RING - 1)
             for half in BOTH:
                 for quarter in BOTH:
                     value = self.total(half, 0, d, quarter)
@@ -299,7 +307,7 @@
             pltpu.VMEM((2, 4, 2 * q, width), BF16), pltpu.VMEM((rows, width), F32)]
 
 
-SEMS = dict(h=1, r=1, g=1, s=1, e=1, q=1, d=1, o=1, ty=1, gate=10, up=5, down=10, proj=10, ag1=32, rs1=48, rs2=48, pair=RING,
+SEMS = dict(h=1, r=1, g=1, s=1, e=1, q=1, d=1, o=1, ty=1, gate=10, up=5, down=10, proj=10, ag1=32, rs1=52, rs2=52, pair=RING,
             local=13, send=22)
 
 
@@ -587,10 +595,10 @@
     w_proj.finish()
 
     def back_projection(k, carry):
-        x2[chunk(k, 256)] = dot(eq_t[:, chunk(k, 256)], wqkv_all[...], TN).astype(BF16)
+        x2[chunk(k, ROWS)] = dot(eq_t[:, chunk(k, ROWS)], wqkv_all[...], TN).astype(BF16)
         return carry
 
-    lax.fori_loop(0, 4, back_projection, 0)
+    lax.fori_loop(0, RING, back_projection, 0)
     gather.step_forward(3)
     gather.step_forward(1)
     w_up.forward()
@@ -606,7 +614,7 @@
     w_up.finish()
 
     def gate_up(k, carry):
-        rows = chunk(k, 256)
+        rows = chunk(k, ROWS)
         both = dot(n_all[rows], wgu[...], NN).astype(BF16)
         ab[rows] = both
         gate = both[:, :ffn].astype(F32)
@@ -614,7 +622,7 @@
         return carry
 
     def down(k):
-        x1[chunk(k, 256)] = dot(u[chunk(k, 256)], wd_all[...], NN).astype(BF16)
+        x1[chunk(k, ROWS)] = dot(u[chunk(k, ROWS)], wd_all[...], NN).astype(BF16)
 
     lax.fori_loop(0, 2, gate_up, 0)
     w_down.forward()
@@ -663,7 +671,7 @@
     ag_e.finish()
 
     def grad_act(k, carry):
-        rows = chunk(k, 256)
+        rows = chunk(k, ROWS)
         grad = dot(e_all[rows], wd_all[...], NT)
         gate = ab[rows, :ffn].astype(F32)
         up = ab[rows, ffn:].astype(F32)
@@ -673,10 +681,10 @@
         return carry
 
     def grad_norm(k):
-        x3[chunk(k, 256)] = dot(ab[chunk(k, 256)], wgu[...], NT).astype(BF16)
+        x3[chunk(k, ROWS)] = dot(ab[chunk(k, ROWS)], wgu[...], NT).astype(BF16)
 
     def project(k, carry):
-        value = dot(wqkv_all[...], n2_all[chunk(k, 256)], NT).astype(BF16)
+        value = dot(wqkv_all[...], n2_all[chunk(k, ROWS)], NT).astype(BF16)
         qkv_send[2 * k] = value[:, :tile]
         qkv_send[2 * k + 1] = value[:, tile:]
         return carry
@@ -685,7 +693,7 @@
     down_grad.start()
     ag_n.step_first()
     down_grad.pair()
-    lax.fori_loop(0, 4, grad_act, 0)
+    lax.fori_loop(0, RING, grad_act, 0)
     ag_n.step_second()
     gate_grad.start()
     down_grad.relay()
@@ -694,20 +702,28 @@
     ag_n.step_forward(1)
     gate_grad.pair()
     ag_n.step_forward(2)
-    rs3.fill(grad_norm)
-    down_grad.finish()
+    rs3.fill(grad_norm, ORDER[:1])
     ag_n.finish()
     ex_e.done()
-    lax.fori_loop(0, 4, project, 0)
+    lax.fori_loop(0, RING, project, 0)
+    rs3.relays(2)
+    rs3.direct(3)
     ex_q.send()
     ex_q.own()
+    rs3.relays(3)
+    rs3.direct(1)
     gate_grad.relay()
     proj_grad.start()
-    rs3.relays(*ORDER)
+    rs3.middle(2)
+    rs3.relays(1)
+    rs3.direct(0)
+    rs3.relays(0)
     proj_grad.pair()
-    rs3.middle(*ORDER)
+    down_grad.finish()
+    rs3.middle(3, 1)
+    rs3.last_relay()
+    rs3.middle(0)
     gate_grad.finish()
-    rs3.last_relay()
     proj_grad.relay()
     rs3.finish()
     inner = 0.0

time: 162 us -> 160 us (0.988)
  Pallas kernels: 161 us -> 159 us
    pallas_call x2, Pallas kernels: 161 us -> 159 us  [call(): pl.pallas_call(kernel, out_shape=[shape_of(shape, dtype) for shape, dtype...]
where the time goes in v2:
time: 160 us
  Pallas kernels  159 us (99%)
    pallas_call x2, Pallas kernels, call(): pl.pallas_call(kernel, out_shape=[shape_of(shape, dtype) for shape, dtype...  159 us

profile of v2, /device:TPU:1, one launch (start us, length us, event | category | flops | bytes accessed | tf_op | source)
XLA Modules:
  0.0 159.8 jit_solution(6880315819037935853)
XLA Ops:
  0.6 157.3 %main_kernel.1 = (bf16[8,64,256]{2,1,0:T(8,128)(2,1)S(1)}, bf16[8,64,256]{2,1,0:T(8,128)(2,1)S(1)}, bf16[128,1024]{1,0:T(8,128)(2,1)S(1)}, bf16[64,1024]{1,0:T(8...) custom-call(bf16[8,64,256]{2,1,0:T(8,128)(2,1)} %bitcast.31, ...), custom_call_target="tpu_custom_call" | custom-call | tf_op jit(solution)/shard_map/main_kernel/pallas_call | solution.py:798
  158.0 1.6 %store_kernel.1 = (bf16[8,64,256]{2,1,0:T(8,128)(2,1)}, bf16[8,64,256]{2,1,0:T(8,128)(2,1)}, bf16[128,1024]{1,0:T(8,128)(2,1)}, bf16[64,1024]{1,0:T(8,128)(2,1)}...) custom-call(bf16[8,64,256]{2,1,0:T(8,128)(2,1)S(1)} %get-tuple-eleme, ...), custom_call_target="tpu_custom_call" | custom-call | tf_op jit(solution)/shard_map/store_kernel/pallas_call | solution.py:798

commit v3 on v2

--- a/solution.py
+++ b/solution.py
@@ -224,22 +224,12 @@
             self.go(src, self.got.at[n * 6 + kind], self.semaphore(half, phase, d, kind), self.place.peer(self.axes(half, phase)[0], 1 - 2 * (kind % 2)))
 
     def semaphore(self, half, phase, d, kind):
-        if phase:
-            return half * 26 + 20 + kind
-        if kind in LATE:
-            return half * 26 + TY + kind - (2 if d == ORDER[0] else 0)
-        return half * 26 + 4 * d + kind % 4 + kind // 4 * 2
+        return self.number(half, phase, d) * 6 + kind
 
     def recv(self, half, phase, d, kind):
         ref = self.got.at[self.number(half, phase, d) * 6 + kind]
-        if phase or kind not in LATE:
-            self.wait(ref, self.semaphore(half, phase, d, kind), self.place.sibling)
+        self.wait(ref, self.semaphore(half, phase, d, kind), self.place.sibling)
         return ref[...].astype(F32)
-
-    def directs(self, d, count):
-        for half in BOTH:
-            for kind in LATE:
-                self.wait(self.x.at[pl.ds(0, count * self.q)], self.semaphore(half, 0, d, kind), self.place.sibling)
 
     def relay(self, half, phase, d):
         n = self.number(half, phase, d)
@@ -280,8 +270,6 @@
 
     def middle(self, *ds):
         for d in ds:
-            if d in LATE:
-                self.directs(d, 1 if d == ORDER[0] else RING - 1)
             for half in BOTH:
                 for quarter in BOTH:
                     value = self.total(half, 0, d, quarter)
@@ -307,7 +295,7 @@
             pltpu.VMEM((2, 4, 2 * q, width), BF16), pltpu.VMEM((rows, width), F32)]
 
 
-SEMS = dict(h=1, r=1, g=1, s=1, e=1, q=1, d=1, o=1, ty=1, gate=10, up=5, down=10, proj=10, ag1=32, rs1=52, rs2=52, pair=RING,
+SEMS = dict(h=1, r=1, g=1, s=1, e=1, q=1, d=1, o=1, ty=1, gate=10, up=5, down=10, proj=10, ag1=32, rs1=60, rs2=60, pair=RING,
             local=13, send=22)
 
 

time: 160 us -> 160 us (level)
  no operation moved by 1% of the time
where the time goes in v3:
time: 160 us; the launch traced here: 159 us
  Pallas kernels  159 us (99%)
    pallas_call x2, Pallas kernels, call(): pl.pallas_call(kernel, out_shape=[shape_of(shape, dtype) for shape, dtype...  159 us

profile of v3, /device:TPU:1, one launch (start us, length us, event | category | flops | bytes accessed | tf_op | source)
XLA Modules:
  0.0 159.4 jit_solution(13723352931219789440)
XLA Ops:
  0.6 157.0 %main_kernel.1 = (bf16[8,64,256]{2,1,0:T(8,128)(2,1)S(1)}, bf16[8,64,256]{2,1,0:T(8,128)(2,1)S(1)}, bf16[128,1024]{1,0:T(8,128)(2,1)S(1)}, bf16[64,1024]{1,0:T(8...) custom-call(bf16[8,64,256]{2,1,0:T(8,128)(2,1)} %bitcast.31, ...), custom_call_target="tpu_custom_call" | custom-call | tf_op jit(solution)/shard_map/main_kernel/pallas_call | solution.py:786
  157.6 1.6 %store_kernel.1 = (bf16[8,64,256]{2,1,0:T(8,128)(2,1)}, bf16[8,64,256]{2,1,0:T(8,128)(2,1)}, bf16[128,1024]{1,0:T(8,128)(2,1)}, bf16[64,1024]{1,0:T(8,128)(2,1)}...) custom-call(bf16[8,64,256]{2,1,0:T(8,128)(2,1)S(1)} %get-tuple-eleme, ...), custom_call_target="tpu_custom_call" | custom-call | tf_op jit(solution)/shard_map/store_kernel/pallas_call | solution.py:786
